TPU v7x, 256 devices: a whole 4x4x8 slice. The times are simulated.
256 devices in a mesh: layer: 4 (over z_lo, core), harm: 64 (over y, z_hi, x).
Axes of the slice: x: 4, y: 4, z: 8 (z_hi: 4, z_lo: 2; z = z_hi * 2 + z_lo), core: 2. Of those that a mesh axis runs over, the one named last changes fastest.
Arguments:
- source: bfloat16 [2, 2048, 128], P(None, 'harm'), may hold values from -6 to 6
- transfer: bfloat16 [4, 2, 2048, 2048], P('layer', None, 'harm'), may hold values from -0.09375 to 0.09375
- fields: bfloat16 [4, 2, 2048, 128], P('layer', None, 'harm'), may hold values from -6 to 6
- orders: int32 [2048], replicated, may hold values from 0 to 2047, each once
Outputs:
- gradients: float32 [4, 2, 4096], P('layer', None, 'harm')
- boundary: bfloat16 [4, 2, 2048, 128], P('layer', None, 'harm')
Inputs may be any that keep to these rules, and one draw needn't show every extreme that they name: `orders`: every value from 0 to 2047 appears exactly once.
All inputs are finite; a program needn't handle non-finite values.
Results may differ from a plain program's by a relative error of at most 0.006.
Values may be sent and summed in bfloat16 or wider, within the bound.
A program may use at most 64 MiB of HBM per device.

v0:
```python
import math
import jax
import jax.numpy as jnp
from jax import lax
from jax.sharding import PartitionSpec as P


def in_order(blocks, dim):
    blocks = jnp.moveaxis(blocks, 0, dim)
    dims = blocks.shape
    return blocks.reshape(*dims[:dim], dims[dim] * dims[dim + 1], *dims[dim + 2 :])


def from_everyone(value, axis):
    copies = jnp.broadcast_to(value, (lax.axis_size(axis), *value.shape))
    return lax.all_to_all(copies, axis, split_axis=0, concat_axis=0, tiled=True)


def gather_directly(value, axis, dim):
    return in_order(from_everyone(value, axis), dim)


def shifted(value, axis, steps):
    count = lax.axis_size(axis)
    first, last = (max(0, -steps), min(count, count - steps))
    return lax.ppermute(value, axis, [(source, source + steps) for source in range(first, last)])


def correlate(adjoint, forward, position, band_start, band_width):
    harmonics = adjoint.shape[1]
    columns = adjoint.shape[2]
    adj_sorted = jnp.take(adjoint, position, axis=1)
    fwd_sorted = jnp.take(forward, position, axis=1)
    padded = jnp.pad(adj_sorted, ((0, 0), (harmonics, harmonics + 1), (0, 0)))
    window_slab = lax.dynamic_slice_in_dim(padded, band_start + 1, harmonics + band_width, 1)
    count = harmonics // band_width
    blocks = window_slab.reshape(2, count + 1, band_width, columns)
    windows = jnp.concatenate([blocks[:, :-1], blocks[:, 1:]], axis=2)
    forward_blocks = fwd_sorted.reshape(2, count, band_width, columns)

    def product(left_part, right_part):
        return jnp.einsum("nkb,ncb->nkc", left_part, right_part, preferred_element_type=jnp.float32)

    real_part = product(forward_blocks[0], windows[0]) - product(forward_blocks[1], windows[1])
    imag_part = product(forward_blocks[0], windows[1]) + product(forward_blocks[1], windows[0])

    def diagonals(result_block):
        flattened = result_block.reshape(count, band_width * 2 * band_width)
        flattened = jnp.pad(flattened, ((0, 0), (0, band_width)))
        shaped = flattened.reshape(count, band_width, 2 * band_width + 1)[:, :, :band_width]
        return jnp.sum(shaped, axis=(0, 1))

    return jnp.stack([diagonals(real_part), diagonals(imag_part)])


def gather_rows(adjoint):
    return lax.all_gather(adjoint, "harm", axis=1, tiled=True)


def spread_fields(local_fields):
    return gather_directly(local_fields, "harm", 2)


def propagate(matrix, gathered):
    real_part = jnp.dot(matrix[0], gathered[0], preferred_element_type=jnp.float32) - jnp.dot(
        matrix[1], gathered[1], preferred_element_type=jnp.float32
    )
    imag_part = jnp.dot(matrix[0], gathered[1], preferred_element_type=jnp.float32) + jnp.dot(
        matrix[1], gathered[0], preferred_element_type=jnp.float32
    )
    return jnp.stack([real_part, imag_part]).astype(jnp.bfloat16)


def per_device(source, transfer, fields, orders):
    harmonics = orders.shape[0]
    sections = lax.axis_size("layer")
    section_index = lax.axis_index("layer")
    band_width = 2 * harmonics // lax.axis_size("harm")
    band_start = lax.axis_index("harm") * band_width
    rows_dev = transfer.shape[2]
    columns = source.shape[2]
    norm_scale = 1.0 / math.sqrt(harmonics * columns)
    position = (
        jnp.zeros((harmonics,), jnp.int32).at[orders].set(jnp.arange(harmonics, dtype=jnp.int32))
    )
    layers_here = transfer.shape[0]
    field_source = spread_fields(fields)
    micro_count = 1
    micro_cols = columns // micro_count
    stored = jnp.zeros((layers_here, 2, harmonics, columns), jnp.bfloat16)
    bottom = jnp.zeros((2, rows_dev, columns), jnp.bfloat16)
    incoming = jnp.zeros((2, rows_dev, micro_cols), jnp.bfloat16)
    total_steps = sections + micro_count - 1
    for step_index in range(total_steps):
        micro_index = step_index - (sections - 1 - section_index)
        active = (micro_index >= 0) & (micro_index < micro_count)
        if step_index < micro_count:
            top_source = source
        else:
            top_source = jnp.zeros_like(incoming)
        adjoint = jnp.where(section_index == sections - 1, top_source, incoming)
        gathered = gather_rows(adjoint)
        stored = stored.at[0].set(jnp.where(active, gathered, stored[0]))
        adjoint = propagate(transfer[0], gathered)
        bottom = jnp.where(active, adjoint, bottom)
        if step_index < total_steps - 1:
            incoming = shifted(adjoint, "layer", -1)
    grads = jnp.stack(
        [correlate(stored[0], field_source[0], position, band_start, band_width) * norm_scale]
    )
    return (grads, bottom[None])


def solution(mesh):
    return jax.shard_map(
        per_device,
        mesh=mesh,
        in_specs=(
            P(None, "harm", None),
            P("layer", None, "harm", None),
            P("layer", None, "harm", None),
            P(),
        ),
        out_specs=(P("layer", None, "harm"), P("layer", None, "harm", None)),
        check_vma=False,
    )
```

profile of v0, /device:TPU:8, one launch (start us, length us, event | category | flops | bytes accessed | tf_op | source)
XLA Modules:
  0.0 404.4 jit_solution(10969838108467156854)
XLA Ops:
  7.2 0.6 broadcast_select_fusion.5
  7.8 0.1 all-gather.5.cloned.1.call-update
  7.9 0.0 all-gather.7.cloned.1.call-start
  8.0 81.3 %all-gather.5.cloned.1.call-done = bf16[2,2048,128]{2,1,0:T(8,128)(2,1)} async-done(((bf16[2,32,128]{2,1,0:T(8,128)(2,1)}), bf16[2,2048,128]{2,1,0:T(8,128)(2,1)}) %all-gather.5.cloned.1.call-update) | async-done | bytes 1048592 | tf_op jit(solution)/shard_map/all_gather | solution.py:57
  89.2 1.4 fusion.15
  90.6 1.3 fusion.16
  92.0 1.3 fusion
  93.3 0.2 fusion.1
  93.5 1.3 collective-permute-start
  94.8 1.8 collective-permute-done
  96.6 0.6 broadcast_select_fusion.4
  97.2 0.0 all-gather.9.cloned.1.call-start
  97.3 72.2 %all-gather.7.cloned.1.call-done = bf16[2,2048,128]{2,1,0:T(8,128)(2,1)} async-done(((bf16[2,32,128]{2,1,0:T(8,128)(2,1)}), bf16[2,2048,128]{2,1,0:T(8,128)(2,1)}) %all-gather.7.cloned.1.call-update) | async-done | bytes 1048592 | tf_op jit(solution)/shard_map/all_gather | solution.py:57
  169.5 1.3 fusion.18
  170.9 1.2 fusion.17
  172.1 1.3 fusion.2
  173.4 0.2 fusion.3
  173.6 1.3 collective-permute-start.1
  174.9 1.8 collective-permute-done.1
  176.7 0.6 broadcast_select_fusion.3
  177.3 72.3 %all-gather.9.cloned.1.call-done = bf16[2,2048,128]{2,1,0:T(8,128)(2,1)} async-done(((bf16[2,32,128]{2,1,0:T(8,128)(2,1)}), bf16[2,2048,128]{2,1,0:T(8,128)(2,1)}) %all-gather.9.cloned.1.call-update) | async-done | bytes 1048592 | tf_op jit(solution)/shard_map/all_gather | solution.py:57
  249.6 1.3 fusion.20
  250.9 1.2 fusion.19
  252.2 1.3 fusion.4
  253.5 0.2 fusion.5
  253.7 1.3 collective-permute-start.2
  255.0 1.2 broadcast_in_dim.17
  256.3 8.7 %all-to-all-start = ((bf16[64,1,2,32,128]{4,3,2,1,0:T(8,128)(2,1)}), bf16[64,1,2,32,128]{4,3,2,1,0:T(8,128)(2,1)S(1)}, u32[]{:S(2)}, u32[]{:S(2)}) async-start(bf16[64,1,2,32,128]{4,3,2,1,0:T(8,128)(2,1)} %broadcast_in_dim.17), calls=%async_computation | async-start | bytes 2097152 | tf_op jit(solution)/shard_map/all_to_all | solution.py:16
  264.9 0.0 all-gather.11.cloned.1.call-start
  265.0 0.6 broadcast_select_fusion.2
  265.7 8.2 %scatter_custom_fusion = s32[2048]{0:T(1024)S(1)} fusion(s32[2048]{0:T(1024)S(1)} %compare_select_fusion.1, s32[2048]{0:T(1024)S(1)} %iota.3, s32[]{:T(128)} %constant.110.clone.1), kind=kCustom, calls=%fused_computation.103 | custom fusion | bytes 8196 | tf_op jit(solution)/shard_map/scatter | solution.py:84
  274.0 21.0 %all-to-all-done = bf16[64,1,2,32,128]{4,3,2,1,0:T(8,128)(2,1)S(1)} async-done(((bf16[64,1,2,32,128]{4,3,2,1,0:T(8,128)(2,1)}), bf16[64,1,2,32,128]{4,3,2,1,0:T(8,128)(2,1)S(1)}, u32[]{:S(2)}, u32[]{:S(2)}) %all-to-all-start) | async-done | bytes 1048608 | tf_op jit(solution)/shard_map/all_to_all | solution.py:16
  295.0 0.1 copy.12
  295.1 8.7 %copy.13 = bf16[2,2048,128]{2,0,1:T(2,128)(2,1)S(1)} copy(bf16[2,2048,128]{2,1,0:T(8,128)(2,1)S(1)} %bitcast.145) | data formatting | bytes 2097152 | tf_op jit(solution)/shard_map/squeeze;reshape | solution.py:109
  303.8 7.1 %gather_fusion = bf16[2048,2,128]{2,1,0:T(2,128)(2,1)S(1)} fusion(bf16[2,2048,128]{2,0,1:T(2,128)(2,1)S(1)} %copy.13, s32[2048]{0:T(1024)S(1)} %fusion.58), kind=kCustom, calls=%fused_computation.clone | custom fusion | bytes 2105344 | tf_op jit(solution)/shard_map/jit(_take)/gather | solution.py:33
  310.8 36.5 %all-gather.11.cloned.1.call-done = bf16[2,2048,128]{2,1,0:T(8,128)(2,1)} async-done(((bf16[2,32,128]{2,1,0:T(8,128)(2,1)}), bf16[2,2048,128]{2,1,0:T(8,128)(2,1)}) %all-gather.11.cloned.1.call-update) | async-done | bytes 1048592 | tf_op jit(solution)/shard_map/all_gather | solution.py:57
  347.4 1.4 select_select_fusion
  348.8 8.7 %copy.14 = bf16[2,2048,128]{2,0,1:T(2,128)(2,1)S(1)} copy(bf16[2,2048,128]{2,1,0:T(8,128)(2,1)S(1)} %select_select_fusion) | data formatting | bytes 2097152 | tf_op jit(solution)/shard_map/jit(_where)/select_n | solution.py:103
  357.5 7.1 %gather_fusion.1 = bf16[2048,2,128]{2,1,0:T(2,128)(2,1)S(1)} fusion(bf16[2,2048,128]{2,0,1:T(2,128)(2,1)S(1)} %copy.14, s32[2048]{0:T(1024)S(1)} %fusion.58), kind=kCustom, calls=%fused_computation.1.clone | custom fusion | bytes 2105344 | tf_op jit(solution)/shard_map/jit(_take)/gather | solution.py:32
  364.5 7.6 %fusion.14 = (bf16[2,2048,128]{2,0,1:T(2,128)(2,1)S(1)}, bf16[2,2048,128]{2,0,1:T(2,128)(2,1)S(1)}) fusion(bf16[2048,2,128]{2,1,0:T(2,128)(2,1)S(1)} %gather_fusion.1, pred[2048]{0:T(1024)(128)(4,1)S(1)} %compare_and_fusion, bf16[2048,2,128]{2,1,0:T(2,128)(2,1)S(1)} %gather_fusion), kind=kLoop, calls=%fused_computation.38 | loop fusion | flops 1048576 | bytes 4196352 | tf_op jit(solution)/shard_map/jit(_take)/select_n | solution.py:32
  372.1 6.4 %pad_dynamic-slice_fusion = bf16[2,2112,128]{2,0,1:T(2,128)(2,1)S(1)} fusion(s32[]{:T(128)S(6)} %select_n.125, bf16[2,2048,128]{2,0,1:T(2,128)(2,1)S(1)} %get-tuple-element.55), kind=kLoop, calls=%fused_computation.3 | loop fusion | bytes 2129924 | tf_op jit(solution)/shard_map/dynamic_slice | solution.py:35
  378.6 0.1 copy.15
  378.7 0.6 fusion.66
  379.3 1.5 fusion.67
  380.8 0.1 copy.16
  380.9 0.8 fusion.23
  381.7 0.8 fusion.64
  382.6 0.1 copy.17
  382.6 0.8 convolution_add_fusion
  383.5 0.6 copy.22
  384.1 0.8 convolution_subtract_fusion
  384.9 0.6 copy.23
  385.5 0.1 pad.21
  385.6 1.1 pad.20
  386.7 3.8 reshape.351
  390.4 0.3 slice_reduce_fusion.1
  390.7 2.7 reshape.353
  393.5 0.3 slice_reduce_fusion
  393.7 0.6 maximum_multiply_fusion
  394.3 1.2 fusion.22
  395.6 1.2 fusion.21
  396.8 0.2 fusion.9
  397.0 0.2 fusion.8
  397.2 0.6 maximum_select_fusion
  (26 shorter events, 0.2 us)
Async XLA Ops:
  7.2 86.1 %copy-start.6 = (bf16[1,2,32,2048]{3,2,1,0:T(8,128)(2,1)S(1)}, bf16[1,2,32,2048]{3,2,1,0:T(8,128)(2,1)}, u32[]{:S(2)}) copy-start(bf16[1,2,32,2048]{3,2,1,0:T(8,128)(2,1)} %param.15) | copy-start | bytes 786436
  7.2 82.1 %all-gather.5.cloned.1.call-start = ((), (), s32[]{:S(2)}) async-start(), calls=%async_computation.1 | async-start | bytes 1064960 | tf_op jit(solution)/shard_map/all_gather | solution.py:57
  7.9 161.6 %all-gather.7.cloned.1.call-start = ((), (), s32[]{:S(2)}) async-start(), calls=%async_computation.2 | async-start | bytes 1064960 | tf_op jit(solution)/shard_map/all_gather | solution.py:57
  89.2 4.1 %copy-start = (bf16[2,2048,128]{2,1,0:T(8,128)(2,1)S(1)}, bf16[2,2048,128]{2,1,0:T(8,128)(2,1)}, u32[]{:S(2)}) copy-start(bf16[2,2048,128]{2,1,0:T(8,128)(2,1)} %all-gather.5.cloned.1.call-done) | copy-start | bytes 3145732
  93.5 3.1 collective-permute-start
  97.2 152.4 %all-gather.9.cloned.1.call-start = ((), (), s32[]{:S(2)}) async-start(), calls=%async_computation.3 | async-start | bytes 1064960 | tf_op jit(solution)/shard_map/all_gather | solution.py:57
  169.5 3.9 copy-start.1
  172.1 82.9 %copy-start.4 = (bf16[1,2,32,128]{3,2,1,0:T(8,128)(2,1)S(1)}, bf16[1,2,32,128]{3,2,1,0:T(8,128)(2,1)}, u32[]{:S(2)}) copy-start(bf16[1,2,32,128]{3,2,1,0:T(8,128)(2,1)} %param.16) | copy-start | bytes 49156
  173.6 3.1 collective-permute-start.1
  249.6 3.8 copy-start.3
  253.5 12.2 %copy-start.5 = (s32[2048]{0:T(1024)S(1)}, s32[2048]{0:T(1024)}, u32[]{:S(2)}) copy-start(s32[2048]{0:T(1024)} %param.17) | copy-start | bytes 24580
  253.7 11.3 %collective-permute-start.2 = (bf16[2,32,128]{2,1,0:T(8,128)(2,1)S(1)}, bf16[2,32,128]{2,1,0:T(8,128)(2,1)S(1)}, u32[]{:S(2)}, u32[]{:S(2)}) collective-permute-start(bf16[2,32,128]{2,1,0:T(8,128)(2,1)S(1)} %pad_maximum_fusion.3), channel_id=1, source_target_pairs={{64,0},{128,64},{192,128},{65,1},{129,65},{193,129},{66,2},{130,66... | collective-permute-start | bytes 49160 | tf_op jit(solution)/shard_map/ppermute | solution.py:26
  256.3 38.7 %all-to-all-start = ((bf16[64,1,2,32,128]{4,3,2,1,0:T(8,128)(2,1)}), bf16[64,1,2,32,128]{4,3,2,1,0:T(8,128)(2,1)S(1)}, u32[]{:S(2)}, u32[]{:S(2)}) async-start(bf16[64,1,2,32,128]{4,3,2,1,0:T(8,128)(2,1)} %broadcast_in_dim.17), calls=%async_computation | async-start | bytes 2097152 | tf_op jit(solution)/shard_map/all_to_all | solution.py:16
  264.9 82.4 %all-gather.11.cloned.1.call-start = ((), (), s32[]{:S(2)}) async-start(), calls=%async_computation.4 | async-start | bytes 1064960 | tf_op jit(solution)/shard_map/all_gather | solution.py:57
  393.4 3.4 copy-start.2
Sparse Core Ops, SparseCore 0:
  11.7 77.4 all-gather.4
  97.4 72.1 all-gather.6
  177.4 72.1 all-gather.8
  269.2 78.1 all-gather.10
where the time goes:
time: 405 us; the launch traced here: 404 us
  waiting for transfers between devices  287 us (71%)
  local copies, waits for them, and re-layouts  58.7 us (14%)
  matrix products  18.4 us (5%)
  between operations  14.2 us (4%)
  other arithmetic  13.3 us (3%)
  starting transfers between devices  12.7 us (3%)
    all_gather x4, waiting for transfers between devices, gather_rows(): return lax.all_gather(adjoint, 'harm', axis=1, tiled=True)  262 us
    all_to_all x1, waiting for transfers between devices, from_everyone(): return lax.all_to_all(copies, axis, split_axis=0, concat_axis=0, tiled=True)  21 us
    all_to_all x1, starting transfers between devices, from_everyone(): return lax.all_to_all(copies, axis, split_axis=0, concat_axis=0, tiled=True)  8.68 us
    another operation x1, local copies, waits for them, and re-layouts, per_device(): field_source[0]  8.68 us
    select_n x1, local copies, waits for them, and re-layouts, per_device(): stored = stored.at[0].set(jnp.where(active, gathered, stored[0]))  8.68 us
    scatter x1, local copies, waits for them, and re-layouts, per_device(): jnp.zeros((harmonics,), jnp.int32).at[orders]  8.23 us
  transfers between devices with their start and end apart: 8, of which 7 were waited for; matrix products, arithmetic and copies ran while one was open for 6% of the time, Pallas kernels for 0%

commit v1 on v0

--- a/solution.py
+++ b/solution.py
@@ -54,7 +54,9 @@
 
 
 def gather_rows(adjoint):
-    return lax.all_gather(adjoint, "harm", axis=1, tiled=True)
+    return jnp.concatenate(
+        lax.all_to_all(jnp.stack([adjoint] * lax.axis_size("harm")), "harm", 0, 0), axis=1
+    )
 
 
 def spread_fields(local_fields):

time: 405 us -> 250 us (0.62)
  waiting for transfers between devices: 287 us -> 30 us
  blocking collectives: 0 us -> 114 us
  between operations: 14.2 us -> 1.14 us
  matrix products: 18.4 us -> 6.59 us
  starting transfers between devices: 12.7 us -> 21.5 us
  local copies, waits for them, and re-layouts: 58.7 us -> 65.3 us
    all_gather x4 -> x0, waiting for transfers between devices: 262 us -> none  [gather_rows(): return lax.all_gather(adjoint, 'harm', axis=1, tiled=True)]
    all_to_all x0 -> x3, blocking collectives: none -> 114 us  [gather_rows(): lax.all_to_all(jnp.stack([adjoint] * lax.axis_size('harm')), 'harm', 0, 0)]
    gather x1, local copies, waits for them, and re-layouts: 7.05 us -> 15 us  [correlate(): fwd_sorted = jnp.take(forward, position, axis=1)]
    all_to_all x0 -> x1, starting transfers between devices: none -> 7.91 us  [gather_rows(): lax.all_to_all(jnp.stack([adjoint] * lax.axis_size('harm')), 'harm', 0, 0)]
    select_n x1, local copies, waits for them, and re-layouts: 8.68 us -> 1.08 us  [per_device(): stored = stored.at[0].set(jnp.where(active, gathered, stored[0]))]
    dot_general x4, matrix products: 5.2 us -> 0.81 us  [propagate(): jnp.dot(matrix[1], gathered[1], preferred_element_type=jnp.float32)]
  transfers between devices with their start and end apart: 8 -> 5, of which waited for: 7 -> 4; matrix products, arithmetic and copies ran while one was open for 6% -> 14% of each run, Pallas kernels for 0% -> 0%
where the time goes in v1:
time: 250 us; the launch traced here: 249 us
  blocking collectives  114 us (46%)
  local copies, waits for them, and re-layouts  65.3 us (26%)
  waiting for transfers between devices  30 us (12%)
  starting transfers between devices  21.5 us (9%)
  other arithmetic  10.9 us (4%)
  matrix products  6.59 us (3%)
    all_to_all x3, blocking collectives, gather_rows(): lax.all_to_all(jnp.stack([adjoint] * lax.axis_size('harm')), 'harm', 0, 0)  114 us
    all_to_all x1, waiting for transfers between devices, from_everyone(): return lax.all_to_all(copies, axis, split_axis=0, concat_axis=0, tiled=True)  22.9 us
    gather x1, local copies, waits for them, and re-layouts, correlate(): fwd_sorted = jnp.take(forward, position, axis=1)  15 us
    all_to_all x1, starting transfers between devices, from_everyone(): return lax.all_to_all(copies, axis, split_axis=0, concat_axis=0, tiled=True)  9.76 us
    another operation x1, local copies, waits for them, and re-layouts, per_device(): field_source[0]  9.45 us
    scatter x1, local copies, waits for them, and re-layouts, per_device(): jnp.zeros((harmonics,), jnp.int32).at[orders]  8.23 us
    all_to_all x1, starting transfers between devices, gather_rows(): lax.all_to_all(jnp.stack([adjoint] * lax.axis_size('harm')), 'harm', 0, 0)  7.91 us
    select_n x1, other arithmetic, correlate(): adj_sorted = jnp.take(adjoint, position, axis=1)  7.59 us
  transfers between devices with their start and end apart: 5, of which 4 were waited for; matrix products, arithmetic and copies ran while one was open for 14% of the time, Pallas kernels for 0%

profile of v1, /device:TPU:8, one launch (start us, length us, event | category | flops | bytes accessed | tf_op | source)
XLA Modules:
  0.0 249.4 jit_solution(94307073561378878)
XLA Ops:
  0.7 0.2 stack.65
  0.9 38.9 %all_to_all.25 = bf16[64,2,32,128]{3,2,1,0:T(8,128)(2,1)S(1)} all-to-all(bf16[64,2,32,128]{3,2,1,0:T(8,128)(2,1)S(1)} %stack.65), channel_id=1, replica_groups=mesh['layer'=4,'harm'=64] {'harm'}, dimensions={0} | all-to-all | bytes 2097152 | tf_op jit(solution)/shard_map/all_to_all | solution.py:58
  39.8 0.1 copy.46
  40.0 0.8 copy-done
  40.8 0.2 fusion.28
  41.0 0.2 fusion.26
  41.2 0.2 fusion.1
  41.4 0.2 fusion
  41.6 1.3 collective-permute-start
  42.9 1.8 collective-permute-done
  44.7 0.2 stack.69
  44.9 36.7 %all_to_all.26 = bf16[64,2,32,128]{3,2,1,0:T(8,128)(2,1)S(1)} all-to-all(bf16[64,2,32,128]{3,2,1,0:T(8,128)(2,1)S(1)} %stack.69), channel_id=1, replica_groups=mesh['layer'=4,'harm'=64] {'harm'}, dimensions={0} | all-to-all | bytes 2097152 | tf_op jit(solution)/shard_map/all_to_all | solution.py:58
  81.6 0.1 copy.45
  81.8 0.2 fusion.32
  82.0 0.2 fusion.30
  82.2 0.2 fusion.3
  82.4 0.2 fusion.2
  82.7 1.3 collective-permute-start.1
  84.0 3.5 %collective-permute-done.1 = bf16[2,32,128]{2,1,0:T(8,128)(2,1)S(1)} collective-permute-done((bf16[2,32,128]{2,1,0:T(8,128)(2,1)S(1)}, bf16[2,32,128]{2,1,0:T(8,128)(2,1)S(1)}, u32[]{:S(2)}, u32[]{:S(2)}) %collective-permute-start.1) | collective-permute-done | bytes 16416 | tf_op jit(solution)/shard_map/ppermute | solution.py:26
  87.5 0.2 stack.73
  87.7 38.3 %all_to_all.27 = bf16[64,2,32,128]{3,2,1,0:T(8,128)(2,1)S(1)} all-to-all(bf16[64,2,32,128]{3,2,1,0:T(8,128)(2,1)S(1)} %stack.73), channel_id=1, replica_groups=mesh['layer'=4,'harm'=64] {'harm'}, dimensions={0} | all-to-all | bytes 2097152 | tf_op jit(solution)/shard_map/all_to_all | solution.py:58
  126.0 1.2 broadcast_in_dim.17
  127.3 9.8 %all-to-all-start = ((bf16[64,1,2,32,128]{4,3,2,1,0:T(8,128)(2,1)}), bf16[64,1,2,32,128]{4,3,2,1,0:T(8,128)(2,1)}, u32[]{:S(2)}, u32[]{:S(2)}) async-start(bf16[64,1,2,32,128]{4,3,2,1,0:T(8,128)(2,1)} %broadcast_in_dim.17), calls=%async_computation | async-start | bytes 2097152 | tf_op jit(solution)/shard_map/all_to_all | solution.py:16
  137.0 0.1 copy.44
  137.2 0.2 fusion.36
  137.4 0.2 fusion.34
  137.6 0.2 fusion.5
  137.8 0.2 fusion.4
  138.0 1.3 collective-permute-start.2
  139.3 1.8 collective-permute-done.2
  141.1 22.9 %all-to-all-done = bf16[64,1,2,32,128]{4,3,2,1,0:T(8,128)(2,1)} async-done(((bf16[64,1,2,32,128]{4,3,2,1,0:T(8,128)(2,1)}), bf16[64,1,2,32,128]{4,3,2,1,0:T(8,128)(2,1)}, u32[]{:S(2)}, u32[]{:S(2)}) %all-to-all-start) | async-done | bytes 1048608 | tf_op jit(solution)/shard_map/all_to_all | solution.py:16
  164.1 1.3 stack.77
  165.3 7.9 %all-to-all-start.4 = ((bf16[64,2,32,128]{3,2,1,0:T(8,128)(2,1)}), bf16[64,2,32,128]{3,2,1,0:T(8,128)(2,1)}, u32[]{:S(2)}, u32[]{:S(2)}) async-start(bf16[64,2,32,128]{3,2,1,0:T(8,128)(2,1)} %stack.77), calls=%async_computation.4 | async-start | bytes 2097152 | tf_op jit(solution)/shard_map/all_to_all | solution.py:58
  173.3 8.2 %scatter_custom_fusion = s32[2048]{0:T(1024)S(1)} fusion(s32[2048]{0:T(1024)S(1)} %compare_select_fusion.1, s32[2048]{0:T(1024)S(1)} %iota.3, s32[]{:T(128)} %constant.110.clone.1), kind=kCustom, calls=%fused_computation.99 | custom fusion | bytes 8196 | tf_op jit(solution)/shard_map/scatter | solution.py:86
  181.6 1.3 copy.15
  182.9 9.5 %copy.16 = bf16[2,2048,128]{2,0,1:T(2,128)(2,1)} copy(bf16[2,2048,128]{2,1,0:T(8,128)(2,1)S(1)} %bitcast.179) | data formatting | bytes 2097152 | tf_op jit(solution)/shard_map/squeeze;reshape | solution.py:111
  192.3 15.0 %gather_fusion = bf16[2048,2,128]{2,1,0:T(2,128)(2,1)} fusion(bf16[2,2048,128]{2,0,1:T(2,128)(2,1)} %copy.16, s32[2048]{0:T(1024)S(1)} %fusion.58), kind=kCustom, calls=%fused_computation.clone | custom fusion | bytes 2105344 | tf_op jit(solution)/shard_map/jit(_take)/gather | solution.py:33
  207.4 1.5 select_select_fusion
  208.9 1.1 copy.21
  210.0 7.1 %gather_fusion.1 = bf16[2048,2,128]{2,1,0:T(2,128)(2,1)S(1)} fusion(bf16[2,2048,128]{2,0,1:T(2,128)(2,1)S(1)} %bitcast.178, s32[2048]{0:T(1024)S(1)} %fusion.58), kind=kCustom, calls=%fused_computation.1.clone | custom fusion | bytes 2105344 | tf_op jit(solution)/shard_map/jit(_take)/gather | solution.py:32
  217.0 7.6 %fusion.14 = (bf16[2,2048,128]{2,0,1:T(2,128)(2,1)S(1)}, bf16[2,2048,128]{2,0,1:T(2,128)(2,1)S(1)}) fusion(bf16[2048,2,128]{2,1,0:T(2,128)(2,1)S(1)} %gather_fusion.1, pred[2048]{0:T(1024)(128)(4,1)S(1)} %compare_and_fusion, bf16[2048,2,128]{2,1,0:T(2,128)(2,1)S(1)} %copy-done.1), kind=kLoop, calls=%fused_computation.42 | loop fusion | flops 1048576 | bytes 4196352 | tf_op jit(solution)/shard_map/jit(_take)/select_n | solution.py:32
  224.6 6.2 %pad_dynamic-slice_fusion = bf16[2,2112,128]{2,0,1:T(2,128)(2,1)S(1)} fusion(s32[]{:T(128)S(6)} %select_n.128, bf16[2,2048,128]{2,0,1:T(2,128)(2,1)S(1)} %get-tuple-element.63), kind=kLoop, calls=%fused_computation.3 | loop fusion | bytes 2129924 | tf_op jit(solution)/shard_map/dynamic_slice | solution.py:35
  230.8 0.1 copy.22
  231.0 0.3 fusion.66
  231.3 1.7 fusion.68
  233.1 0.8 fusion.15
  233.9 0.8 fusion.64
  234.8 1.3 copy.43
  236.2 0.2 fusion.40
  236.4 0.2 fusion.38
  236.6 0.2 fusion.8
  236.8 0.2 fusion.9
  237.0 0.1 copy.24
  237.1 0.9 convolution_add_fusion
  237.9 0.6 copy.41
  238.5 0.9 convolution_subtract_fusion
  239.4 0.6 copy.42
  240.1 1.0 pad.20
  241.1 3.8 %reshape.404 = f32[32,64,129]{2,1,0:T(8,128)S(1)} reshape(f32[32,8256]{1,0:T(8,128)} %pad.20) | data formatting | bytes 2113536 | tf_op jit(solution)/shard_map/reshape | solution.py:50
  244.9 0.3 slice_reduce_fusion.1
  245.2 2.7 %reshape.406 = f32[32,64,129]{2,1,0:T(8,128)S(1)} reshape(f32[32,8256]{1,0:T(8,128)S(1)} %pad.21) | data formatting | bytes 2113536 | tf_op jit(solution)/shard_map/reshape | solution.py:50
  247.9 0.3 slice_reduce_fusion
  248.2 0.6 maximum_multiply_fusion
  248.8 0.6 maximum_select_fusion
  (25 shorter events, 0.5 us)
Async XLA Ops:
  39.8 1.0 copy-start
  41.6 3.1 %collective-permute-start = (bf16[2,32,128]{2,1,0:T(8,128)(2,1)S(1)}, bf16[2,32,128]{2,1,0:T(8,128)(2,1)S(1)}, u32[]{:S(2)}, u32[]{:S(2)}) collective-permute-start(bf16[2,32,128]{2,1,0:T(8,128)(2,1)S(1)} %pad_maximum_fusion.1), channel_id=1, source_target_pairs={{64,0},{128,64},{192,128},{65,1},{129,65},{193,129},{66,2},{130,66... | collective-permute-start | bytes 49160 | tf_op jit(solution)/shard_map/ppermute | solution.py:26
  82.4 43.6 %copy-start.2 = (bf16[1,2,32,128]{3,2,1,0:T(8,128)(2,1)S(1)}, bf16[1,2,32,128]{3,2,1,0:T(8,128)(2,1)}, u32[]{:S(2)}) copy-start(bf16[1,2,32,128]{3,2,1,0:T(8,128)(2,1)} %param.16) | copy-start | bytes 49156
  82.7 4.8 %collective-permute-start.1 = (bf16[2,32,128]{2,1,0:T(8,128)(2,1)S(1)}, bf16[2,32,128]{2,1,0:T(8,128)(2,1)S(1)}, u32[]{:S(2)}, u32[]{:S(2)}) collective-permute-start(bf16[2,32,128]{2,1,0:T(8,128)(2,1)S(1)} %pad_maximum_fusion.2), channel_id=1, source_target_pairs={{64,0},{128,64},{192,128},{65,1},{129,65},{193,129},{66,2},{130,66... | collective-permute-start | bytes 49160 | tf_op jit(solution)/shard_map/ppermute | solution.py:26
  127.3 36.8 %all-to-all-start = ((bf16[64,1,2,32,128]{4,3,2,1,0:T(8,128)(2,1)}), bf16[64,1,2,32,128]{4,3,2,1,0:T(8,128)(2,1)}, u32[]{:S(2)}, u32[]{:S(2)}) async-start(bf16[64,1,2,32,128]{4,3,2,1,0:T(8,128)(2,1)} %broadcast_in_dim.17), calls=%async_computation | async-start | bytes 2097152 | tf_op jit(solution)/shard_map/all_to_all | solution.py:16
  137.8 35.5 %copy-start.3 = (s32[2048]{0:T(1024)S(1)}, s32[2048]{0:T(1024)}, u32[]{:S(2)}) copy-start(s32[2048]{0:T(1024)} %param.17) | copy-start | bytes 24580
  138.0 3.1 %collective-permute-start.2 = (bf16[2,32,128]{2,1,0:T(8,128)(2,1)S(1)}, bf16[2,32,128]{2,1,0:T(8,128)(2,1)S(1)}, u32[]{:S(2)}, u32[]{:S(2)}) collective-permute-start(bf16[2,32,128]{2,1,0:T(8,128)(2,1)S(1)} %pad_maximum_fusion.3), channel_id=1, source_target_pairs={{64,0},{128,64},{192,128},{65,1},{129,65},{193,129},{66,2},{130,66... | collective-permute-start | bytes 49160 | tf_op jit(solution)/shard_map/ppermute | solution.py:26
  165.3 42.0 %all-to-all-start.4 = ((bf16[64,2,32,128]{3,2,1,0:T(8,128)(2,1)}), bf16[64,2,32,128]{3,2,1,0:T(8,128)(2,1)}, u32[]{:S(2)}, u32[]{:S(2)}) async-start(bf16[64,2,32,128]{3,2,1,0:T(8,128)(2,1)} %stack.77), calls=%async_computation.4 | async-start | bytes 2097152 | tf_op jit(solution)/shard_map/all_to_all | solution.py:58
  208.9 8.2 %copy-start.1 = (bf16[2048,2,128]{2,1,0:T(2,128)(2,1)S(1)}, bf16[2048,2,128]{2,1,0:T(2,128)(2,1)}, u32[]{:S(2)}) copy-start(bf16[2048,2,128]{2,1,0:T(2,128)(2,1)} %gather_fusion) | copy-start | bytes 3145732
